TPU v7x, 256 devices: a whole 4x4x8 slice. The times are simulated.
256 devices in a mesh: dp: 32 (over x, z), seq: 8 (over y, core).
Axes of the slice: x: 4, y: 4, z: 8, core: 2. Of those that a mesh axis runs over, the one named last changes fastest.
Arguments:
- hidden: bfloat16 [32, 8192, 4096], P('dp', 'seq'), may hold values from -6 to 6
- value_weight: bfloat16 [4096, 64], replicated, may hold values from -0.09375 to 0.09375
- value_bias: float32 [64], replicated, may hold values from -1 to 1
- returns: float32 [32, 8192], P('dp', 'seq'), may hold values from -12 to 12, as said below
- task_bins: int32 [32, 8192], P('dp', 'seq'), may hold values from 0 to 63
- loss_mask: int32 [32, 8192], P('dp', 'seq'), may hold values 0 or 1
Outputs:
- targets: float32 [32, 8192], P('dp', 'seq')
- weight_grad: float32 [4096, 64], replicated
- bias_grad: float32 [64], replicated
Inputs may be any that keep to these rules, and one draw needn't show every extreme that they name: The returns of one rollout share a level and a trend along positions.
All inputs are finite; a program needn't handle non-finite values.
Results may differ from a plain program's by a relative error of at most 0.00083.
Values sent between devices are 32-bit elements.
A program may use at most 64 MiB of HBM per device.

v0:
```python
import jax
import jax.numpy as jnp
from jax import lax
from jax.sharding import Mesh
from jax.sharding import PartitionSpec as P

DP = ("dp_0", "dp_1")
DP_SEQ = ("dp_0", "dp_1", "seq_0", "seq_1")
SEQ = ("seq_0", "seq_1")


def one_axis_at_a_time(x, axes):
    for axis in axes:
        x = lax.psum(x, axis)
    return x


def in_blocks(x, dim, devices):
    shape = x.shape
    pieces = x.reshape(*shape[:dim], devices, shape[dim] // devices, *shape[dim + 1 :])
    return jnp.moveaxis(pieces, dim, 0)


def sent_and_summed(x, axis, dim):
    devices = lax.axis_size(axis)
    pieces = lax.all_to_all(in_blocks(x, dim, devices), axis, 0, 0, tiled=True)
    return jnp.sum(pieces, axis=0)


def over_pieces(x, axis):
    pieces = lax.all_gather(x, axis)
    return pieces.sum(axis=0)


def in_order(pieces, dim):
    pieces = jnp.moveaxis(pieces, 0, dim)
    shape = pieces.shape
    return pieces.reshape(*shape[:dim], shape[dim] * shape[dim + 1], *shape[dim + 2 :])


def one_gather(arrays, axis, dims):
    ravelled = jnp.concatenate([a.reshape(-1) for a in arrays])
    lines, at, outs = (lax.all_gather(ravelled, axis), 0, [])
    for a, dim in zip(arrays, dims):
        pieces = lines[:, at : at + a.size].reshape(-1, *a.shape)
        outs.append(in_order(pieces, dim))
        at += a.size
    return tuple(outs)


def on_device(hidden, value_weight, value_bias, returns, task_bins, loss_mask):
    rollouts = hidden.shape[0] * lax.axis_size(DP)
    states = hidden.reshape(-1, hidden.shape[2])
    flat_returns = returns.reshape(-1)
    bins_iota = jnp.arange(value_weight.shape[1], dtype=jnp.int32)
    chosen = (task_bins.reshape(-1)[:, None] == bins_iota).astype(jnp.float32)
    valid = loss_mask.reshape(-1).astype(jnp.float32)
    onehot = chosen * valid[:, None]
    scores = jnp.dot(states, value_weight, preferred_element_type=jnp.float32)
    counts = jnp.sum(onehot, axis=0)
    summed = jnp.sum(onehot * flat_returns[:, None], axis=0)
    squares = jnp.sum(onehot * flat_returns[:, None] * flat_returns[:, None], axis=0)
    counts, summed, squares = (
        one_axis_at_a_time(counts, DP_SEQ),
        one_axis_at_a_time(summed, DP_SEQ),
        one_axis_at_a_time(squares, DP_SEQ),
    )
    means = summed / jnp.maximum(counts, 1.0)
    second = squares - summed * means
    floor_counts = jnp.maximum(counts, 1.0)
    spread = jnp.sqrt(second / floor_counts + 0.1)
    deviation = flat_returns[:, None] - means
    targets = jnp.sum(chosen * (deviation / spread), axis=-1)
    predicted = jnp.sum((scores + value_bias) * chosen, axis=-1)
    slope = valid * jnp.clip(predicted - targets, -1.0, 1.0) / rollouts
    coefficient = chosen * slope[:, None]
    weight_grad = lax.dot_general(
        states,
        coefficient.astype(jnp.bfloat16),
        (((0,), (0,)), ((), ())),
        preferred_element_type=jnp.float32,
    )
    bias_grad = jnp.sum(coefficient, axis=0)
    weight_share, bias_share = (
        sent_and_summed(weight_grad, SEQ, 0),
        sent_and_summed(bias_grad, SEQ, 0),
    )
    weight_share, bias_share = (over_pieces(weight_share, DP), over_pieces(bias_share, DP))
    weight_grad, bias_grad = one_gather((weight_share, bias_share), SEQ, (0, 0))
    return (targets.reshape(returns.shape), weight_grad, bias_grad)


def solution(mesh):
    torus = Mesh(mesh.devices.reshape(4, 8, 4, 2), ("dp_0", "dp_1", "seq_0", "seq_1"))
    return jax.shard_map(
        on_device,
        mesh=torus,
        in_specs=(P(DP, SEQ, None), P(), P(), P(DP, SEQ), P(DP, SEQ), P(DP, SEQ)),
        out_specs=(P(DP, SEQ), P(), P()),
        check_vma=False,
    )
```

profile of v0, /device:TPU:2, one launch (start us, length us, event | category | flops | bytes accessed | tf_op | source)
XLA Modules:
  0.0 242.7 jit_solution(15174251492240911007)
XLA Ops:
  7.2 0.0 copy-start
  7.2 0.0 all-gather.5.cloned.1.call-start
  7.2 0.7 convert_element_type.17
  8.0 0.9 fusion.14
  8.9 10.0 %all-reduce.4 = (f32[64]{0:T(128)S(1)}, f32[64]{0:T(128)S(1)}, f32[64]{0:T(128)S(1)}) all-reduce(f32[64]{0:T(128)S(1)} %get-tuple-element.13, f32[64]{0:T(128)S(1)} %get-tuple-element.12, f32[64]{0:T(128)S(1)} %get-tuple-element.14), channel_id=1, replica_groups=mesh['dp_0'=4,'dp_1'=8,'seq_0'=4,'seq_1'=2] {'dp_0'}, use_global_device_ids=true, to_apply=%region_11.0 | all-reduce | flops 192 | bytes 1536 | tf_op jit(solution)/shard_map/psum | solution.py:14
  18.8 18.6 %all-reduce.2 = (f32[64]{0:T(128)S(1)}, f32[64]{0:T(128)S(1)}, f32[64]{0:T(128)S(1)}) all-reduce(f32[64]{0:T(128)S(1)} %get-tuple-element.21, f32[64]{0:T(128)S(1)} %get-tuple-element.22, f32[64]{0:T(128)S(1)} %get-tuple-element.23), channel_id=1, replica_groups=mesh['dp_0'=4,'dp_1'=8,'seq_0'=4,'seq_1'=2] {'dp_1'}, use_global_device_ids=true, to_apply=%region_12.0 | all-reduce | flops 192 | bytes 1536 | tf_op jit(solution)/shard_map/psum | solution.py:14
  37.5 10.7 %all-reduce.3 = (f32[64]{0:T(128)S(1)}, f32[64]{0:T(128)S(1)}, f32[64]{0:T(128)S(1)}) all-reduce(f32[64]{0:T(128)S(1)} %get-tuple-element.15, f32[64]{0:T(128)S(1)} %get-tuple-element.16, f32[64]{0:T(128)S(1)} %get-tuple-element.17), channel_id=1, replica_groups=mesh['dp_0'=4,'dp_1'=8,'seq_0'=4,'seq_1'=2] {'seq_0'}, use_global_device_ids=true, to_apply=%region_13.0 | all-reduce | flops 192 | bytes 1536 | tf_op jit(solution)/shard_map/psum | solution.py:14
  48.2 2.5 %all-reduce.5 = (f32[64]{0:T(128)S(1)}, f32[64]{0:T(128)S(1)}, f32[64]{0:T(128)S(1)}) all-reduce(f32[64]{0:T(128)S(1)} %get-tuple-element.18, f32[64]{0:T(128)S(1)} %get-tuple-element.19, f32[64]{0:T(128)S(1)} %get-tuple-element.20), channel_id=1, replica_groups=mesh['dp_0'=4,'dp_1'=8,'seq_0'=4,'seq_1'=2] {'seq_1'}, use_global_device_ids=true, to_apply=%region_14.0 | all-reduce | flops 192 | bytes 1536 | tf_op jit(solution)/shard_map/psum | solution.py:14
  50.7 0.8 select_reduce_fusion.2
  51.5 0.0 copy-done
  51.5 0.0 copy-start.4
  51.6 0.0 copy-start.1
  51.6 0.0 copy-start.3
  51.6 6.2 %fusion.10 = f32[1024]{0:T(1024)S(1)} fusion(bf16[4096,64]{0,1:T(8,128)(2,1)S(1)} %copy-done, bf16[1,1024,4096]{2,1,0:T(8,128)(2,1)} %param.6, f32[64]{0:T(128)} %param.8, s32[1024]{0:T(1024)} %bitcast.34), kind=kOutput, calls=%fused_computation.7 | convolution fusion | flops 537132032 | bytes 8921344 | tf_op jit(solution)/shard_map/dot_general | solution.py:59
  57.9 1.6 fusion
  59.4 0.0 copy-start.6
  59.4 0.0 copy-start.5
  59.5 0.1 copy.23
  59.5 18.4 %all_to_all.14 = f32[8,512,64]{1,2,0:T(8,128)S(1)} all-to-all(f32[8,512,64]{1,2,0:T(8,128)S(1)} %bitcast.30), channel_id=1, replica_groups=mesh['dp_0'=4,'dp_1'=8,'seq_0'=4,'seq_1'=2] {'seq_0','seq_1'}, dimensions={0} | all-to-all | bytes 2097152 | tf_op jit(solution)/shard_map/all_to_all | solution.py:26
  77.9 0.7 reduce_sum.95
  78.7 0.0 all-gather.5.cloned.1.call-update
  78.7 0.1 select_reduce_fusion
  78.8 0.7 all_to_all.10
  79.5 3.3 %all-to-all-start.1 = ((f32[8,1,8]{2,1,0:T(1,128)}), f32[8,1,8]{2,1,0:T(1,128)S(1)}, u32[]{:S(2)}, u32[]{:S(2)}) async-start(f32[8,1,8]{2,1,0:T(1,128)} %bitcast.6), calls=%async_computation.1 | async-start | bytes 8192 | tf_op jit(solution)/shard_map/all_to_all | solution.py:26
  82.8 0.0 all-reduce.8.cloned.1.call-start
  82.8 0.0 copy-done.6
  82.8 0.6 dynamic-slice.1
  83.4 0.6 dynamic-slice
  85.3 2.7 %all-to-all-done.1 = f32[8,1,8]{2,1,0:T(1,128)S(1)} async-done(((f32[8,1,8]{2,1,0:T(1,128)}), f32[8,1,8]{2,1,0:T(1,128)S(1)}, u32[]{:S(2)}, u32[]{:S(2)}) %all-to-all-start.1) | async-done | bytes 288 | tf_op jit(solution)/shard_map/all_to_all | solution.py:26
  88.0 0.2 dynamic-update-slice
  88.2 62.2 %all-reduce = f32[256]{0:T(256)S(1)} all-reduce(f32[256]{0:T(256)S(1)} %dynamic-update-slice), channel_id=3, replica_groups=mesh['dp_0'=4,'dp_1'=8,'seq_0'=4,'seq_1'=2] {'dp_0','dp_1'}, use_global_device_ids=true, to_apply=%add | all-reduce | flops 256 | bytes 2048
  150.4 0.1 reshape.54
  150.5 4.8 %all-gather.5.cloned.1.call-done = f32[16384,64]{0,1:T(8,128)} async-done(((f32[512,64]{0,1:T(8,128)}), f32[16384,64]{0,1:T(8,128)}) %all-gather.5.cloned.1.call-update) | async-done | bytes 4194320 | tf_op jit(solution)/shard_map/all_gather | solution.py:31
  155.4 4.6 %copy.21 = f32[8,8,32,512]{3,2,1,0:T(8,128)S(1)} copy(f32[8,8,32,512]{3,1,2,0:T(8,128)} %bitcast.29) | data formatting | bytes 8388608
  159.9 0.7 bitcast_reduce_fusion
  160.6 0.1 copy.16
  160.7 0.1 reshape.51
  160.8 0.1 broadcast.28
  160.9 0.5 maximum_dynamic-update-slice_fusion
  161.4 0.0 copy-start.2
  161.5 1.0 copy-done.2
  162.5 0.0 all-reduce.8.cloned.1.call-update
  162.5 66.3 %all-reduce.8.cloned.1.call-done = f32[262208]{0:T(1024)} async-done(((f32[262208]{0:T(1024)}), f32[262208]{0:T(1024)}) %all-reduce.8.cloned.1.call-update) | async-done | bytes 1048848
  228.8 1.8 reshape.55
  230.6 1.0 slice.8
  231.6 0.6 reshape.52
  232.2 2.1 reshape_reshape.3
  234.3 1.6 copy.18
  (10 shorter events, 0.1 us)
Async XLA Ops:
  7.2 44.4 %copy-start = (bf16[4096,64]{0,1:T(8,128)(2,1)S(1)}, bf16[4096,64]{0,1:T(8,128)(2,1)}, u32[]{:S(2)}) copy-start(bf16[4096,64]{0,1:T(8,128)(2,1)} %param.7) | copy-start | bytes 1572868
  7.2 148.2 %all-gather.5.cloned.1.call-start = ((), (), s32[]{:S(2)}) async-start(), calls=%async_computation.2 | async-start | bytes 4325376 | tf_op jit(solution)/shard_map/all_gather | solution.py:31
  51.5 6.3 %copy-start.4 = (f32[1024]{0:T(1024)}, f32[1024]{0:T(1024)S(1)}, u32[]{:S(2)}) copy-start(f32[1024]{0:T(1024)S(1)} %select_reduce_fusion.2) | copy-start | bytes 12292
  51.6 6.3 %copy-start.1 = (bf16[1,1024,4096]{2,1,0:T(8,128)(2,1)S(1)}, bf16[1,1024,4096]{2,1,0:T(8,128)(2,1)}, u32[]{:S(2)}) copy-start(bf16[1,1024,4096]{2,1,0:T(8,128)(2,1)} %param.6) | copy-start | bytes 25165828
  51.6 6.3 %copy-start.3 = (s32[1,1024]{1,0:T(1,128)S(1)}, s32[1,1024]{1,0:T(1,128)}, u32[]{:S(2)}) copy-start(s32[1,1024]{1,0:T(1,128)} %param.10) | copy-start | bytes 12292
  59.4 23.4 %copy-start.6 = (u32[256]{0:T(256)S(1)}, u32[256]{0:T(256)}, u32[]{:S(2)}) copy-start(u32[256]{0:T(256)} %constant.27) | copy-start | bytes 3076
  59.4 24.0 %copy-start.5 = (u32[256]{0:T(256)S(1)}, u32[256]{0:T(256)}, u32[]{:S(2)}) copy-start(u32[256]{0:T(256)} %constant.22) | copy-start | bytes 3076
  79.5 8.5 %all-to-all-start.1 = ((f32[8,1,8]{2,1,0:T(1,128)}), f32[8,1,8]{2,1,0:T(1,128)S(1)}, u32[]{:S(2)}, u32[]{:S(2)}) async-start(f32[8,1,8]{2,1,0:T(1,128)} %bitcast.6), calls=%async_computation.1 | async-start | bytes 8192 | tf_op jit(solution)/shard_map/all_to_all | solution.py:26
  82.8 146.0 %all-reduce.8.cloned.1.call-start = ((), (), s32[]{:S(2)}) async-start(), calls=%async_computation.3 | async-start | bytes 2105344
  161.4 1.0 copy-start.2
Sparse Core Ops, SparseCore 0:
  78.8 76.5 all-gather.4
  162.6 66.0 all-reduce.7
where the time goes:
time: 243 us
  blocking collectives  122 us (50%)
  waiting for transfers between devices  73.8 us (30%)
  between operations  15.5 us (6%)
  local copies, waits for them, and re-layouts  15.2 us (6%)
  matrix products  7.79 us (3%)
  other arithmetic  4.6 us (2%)
  starting transfers between devices  3.34 us (1%)
    unnamed x3, waiting for transfers between devices  66.3 us
    unnamed x1, blocking collectives  62.2 us
    psum x4, blocking collectives, one_axis_at_a_time(): x = lax.psum(x, axis)  41.8 us
    all_to_all x1, blocking collectives, sent_and_summed(): pieces = lax.all_to_all(in_blocks(x, dim, devices), axis, 0, 0, tiled=True)  18.4 us
    unnamed x21, local copies, waits for them, and re-layouts  8.7 us
    dot_general x1, matrix products, on_device(): scores = jnp.dot(states, value_weight, preferred_element_type=jnp.float32)  6.22 us
  transfers between devices with their start and end apart: 3, of which 3 were waited for; matrix products, arithmetic and copies ran while one was open for 1% of the time, Pallas kernels for 0%

commit v1 on v0

--- a/solution.py
+++ b/solution.py
@@ -11,7 +11,7 @@
 
 def one_axis_at_a_time(x, axes):
     for axis in axes:
-        x = lax.psum(x, axis)
+        x = jnp.sum(lax.all_gather(x, axis), axis=0)
     return x
 
 

time: 243 us -> 255 us (1.049)
  local copies, waits for them, and re-layouts: 15.2 us -> 24 us
  between operations: 15.5 us -> 18.2 us
    unnamed x1 -> x5, blocking collectives: 62.2 us -> 104 us
    psum x4 -> x0, blocking collectives: 41.8 us -> none  [one_axis_at_a_time(): x = lax.psum(x, axis)]
    unnamed x21 -> x49, local copies, waits for them, and re-layouts: 8.7 us -> 16.5 us
where the time goes in v1:
time: 255 us; the launch traced here: 254 us
  blocking collectives  123 us (48%)
  waiting for transfers between devices  73.8 us (29%)
  local copies, waits for them, and re-layouts  24 us (9%)
  between operations  18.2 us (7%)
  matrix products  7.78 us (3%)
  other arithmetic  4.78 us (2%)
  starting transfers between devices  3.34 us (1%)
    unnamed x5, blocking collectives  104 us
    unnamed x3, waiting for transfers between devices  66.3 us
    all_to_all x1, blocking collectives, sent_and_summed(): pieces = lax.all_to_all(in_blocks(x, dim, devices), axis, 0, 0, tiled=True)  18.4 us
    unnamed x49, local copies, waits for them, and re-layouts  16.5 us
    dot_general x1, matrix products, on_device(): scores = jnp.dot(states, value_weight, preferred_element_type=jnp.float32)  6.22 us
  transfers between devices with their start and end apart: 3, of which 3 were waited for; matrix products, arithmetic and copies ran while one was open for 1% of the time, Pallas kernels for 0%

profile of v1, /device:TPU:2, one launch (start us, length us, event | category | flops | bytes accessed | tf_op | source)
XLA Modules:
  0.0 254.5 jit_solution(10965668891434443050)
XLA Ops:
  7.2 1.3 dynamic-slice.3
  8.5 1.3 dynamic-slice.2
  11.1 1.3 dynamic-slice.1
  13.0 1.3 dynamic-slice
  14.9 0.7 convert_element_type.17
  15.6 0.9 fusion.14
  16.6 0.2 dynamic-update-slice.4
  16.8 0.2 dynamic-update-slice
  17.0 0.2 dynamic-update-slice.8
  17.2 9.9 %all-reduce.16 = (f32[256]{0:T(256)S(1)}, f32[256]{0:T(256)S(1)}, f32[256]{0:T(256)S(1)}) all-reduce(f32[256]{0:T(256)S(1)} %dynamic-update-slice.8, f32[256]{0:T(256)S(1)} %dynamic-update-slice, f32[256]{0:T(256)S(1)} %dynamic-update-slice.4), channel_id=10, replica_groups=mesh['dp_0'=4,'dp_1'=8,'seq_0'=4,'seq_1'=2] {'dp_0'}, use_global_device_ids=true, to_apply=%add.8 | all-reduce | flops 768 | bytes 6144
  27.4 0.2 dynamic-update-slice.9
  27.7 0.2 dynamic-update-slice.1
  27.9 0.2 dynamic-update-slice.5
  28.1 18.9 %all-reduce.14 = (f32[512]{0:T(512)S(1)}, f32[512]{0:T(512)S(1)}, f32[512]{0:T(512)S(1)}) all-reduce(f32[512]{0:T(512)S(1)} %dynamic-update-slice.9, f32[512]{0:T(512)S(1)} %dynamic-update-slice.1, f32[512]{0:T(512)S(1)} %dynamic-update-slice.5), channel_id=11, replica_groups=mesh['dp_0'=4,'dp_1'=8,'seq_0'=4,'seq_1'=2] {'dp_1'}, use_global_device_ids=true, to_apply=%add.9 | all-reduce | flops 1536 | bytes 12288
  47.3 0.2 dynamic-update-slice.10
  47.5 0.2 dynamic-update-slice.2
  47.8 0.2 dynamic-update-slice.6
  48.0 10.7 %all-reduce.15 = (f32[256]{0:T(256)S(1)}, f32[256]{0:T(256)S(1)}, f32[256]{0:T(256)S(1)}) all-reduce(f32[256]{0:T(256)S(1)} %dynamic-update-slice.10, f32[256]{0:T(256)S(1)} %dynamic-update-slice.2, f32[256]{0:T(256)S(1)} %dynamic-update-slice.6), channel_id=12, replica_groups=mesh['dp_0'=4,'dp_1'=8,'seq_0'=4,'seq_1'=2] {'seq_0'}, use_global_device_ids=true, to_apply=%add.10 | all-reduce | flops 768 | bytes 6144
  59.0 0.2 dynamic-update-slice.11
  59.3 0.2 dynamic-update-slice.3
  59.5 0.2 dynamic-update-slice.7
  59.7 2.4 all-reduce.17
  62.5 0.8 select_reduce_fusion.2
  63.4 6.2 %fusion.10 = f32[1024]{0:T(1024)S(1)} fusion(bf16[4096,64]{0,1:T(8,128)(2,1)S(1)} %copy-done, bf16[1,1024,4096]{2,1,0:T(8,128)(2,1)} %param.6, f32[64]{0:T(128)} %param.8, s32[1024]{0:T(1024)} %bitcast.38), kind=kOutput, calls=%fused_computation.7 | convolution fusion | flops 537132032 | bytes 8921344 | tf_op jit(solution)/shard_map/dot_general | solution.py:59
  69.6 1.6 fusion
  71.3 18.4 %all_to_all.14 = f32[8,512,64]{1,2,0:T(8,128)S(1)} all-to-all(f32[8,512,64]{1,2,0:T(8,128)S(1)} %bitcast.34), channel_id=1, replica_groups=mesh['dp_0'=4,'dp_1'=8,'seq_0'=4,'seq_1'=2] {'seq_0','seq_1'}, dimensions={0} | all-to-all | bytes 2097152 | tf_op jit(solution)/shard_map/all_to_all | solution.py:26
  89.7 0.7 reduce_sum.215
  90.5 0.1 select_reduce_fusion
  90.6 0.7 all_to_all.10
  91.3 3.3 %all-to-all-start.1 = ((f32[8,1,8]{2,1,0:T(1,128)}), f32[8,1,8]{2,1,0:T(1,128)S(1)}, u32[]{:S(2)}, u32[]{:S(2)}) async-start(f32[8,1,8]{2,1,0:T(1,128)} %bitcast.10), calls=%async_computation.1 | async-start | bytes 8192 | tf_op jit(solution)/shard_map/all_to_all | solution.py:26
  94.6 0.6 dynamic-slice.13
  95.2 0.6 dynamic-slice.12
  97.1 2.7 %all-to-all-done.1 = f32[8,1,8]{2,1,0:T(1,128)S(1)} async-done(((f32[8,1,8]{2,1,0:T(1,128)}), f32[8,1,8]{2,1,0:T(1,128)S(1)}, u32[]{:S(2)}, u32[]{:S(2)}) %all-to-all-start.1) | async-done | bytes 288 | tf_op jit(solution)/shard_map/all_to_all | solution.py:26
  99.8 0.2 dynamic-update-slice.12
  100.0 62.2 %all-reduce.12 = f32[256]{0:T(256)S(1)} all-reduce(f32[256]{0:T(256)S(1)} %dynamic-update-slice.12), channel_id=15, replica_groups=mesh['dp_0'=4,'dp_1'=8,'seq_0'=4,'seq_1'=2] {'dp_0','dp_1'}, use_global_device_ids=true, to_apply=%add.12 | all-reduce | flops 256 | bytes 2048
  162.3 4.8 %all-gather.17.cloned.1.call-done = f32[16384,64]{0,1:T(8,128)} async-done(((f32[512,64]{0,1:T(8,128)}), f32[16384,64]{0,1:T(8,128)}) %all-gather.17.cloned.1.call-update) | async-done | bytes 4194320 | tf_op jit(solution)/shard_map/all_gather | solution.py:31
  167.2 4.6 %copy.26 = f32[8,8,32,512]{3,2,1,0:T(8,128)S(1)} copy(f32[8,8,32,512]{3,1,2,0:T(8,128)} %bitcast.33) | data formatting | bytes 8388608
  171.7 0.7 bitcast_reduce_fusion
  172.4 0.1 copy.21
  172.5 0.1 reshape.66
  172.7 0.5 maximum_dynamic-update-slice_fusion
  173.2 1.0 copy-done.2
  174.3 66.3 %all-reduce.20.cloned.1.call-done = f32[262208]{0:T(1024)} async-done(((f32[262208]{0:T(1024)}), f32[262208]{0:T(1024)}) %all-reduce.20.cloned.1.call-update) | async-done | bytes 1048848
  240.6 1.8 reshape.82
  242.4 1.0 slice.8
  243.4 0.6 reshape.67
  244.0 2.1 reshape_reshape.3
  246.1 1.6 copy.23
  (62 shorter events, 1.7 us)
Async XLA Ops:
  7.2 56.2 %copy-start = (bf16[4096,64]{0,1:T(8,128)(2,1)S(1)}, bf16[4096,64]{0,1:T(8,128)(2,1)}, u32[]{:S(2)}) copy-start(bf16[4096,64]{0,1:T(8,128)(2,1)} %param.7) | copy-start | bytes 1572868
  7.2 160.0 %all-gather.17.cloned.1.call-start = ((), (), s32[]{:S(2)}) async-start(), calls=%async_computation.2 | async-start | bytes 4325376 | tf_op jit(solution)/shard_map/all_gather | solution.py:31
  63.3 6.3 %copy-start.4 = (f32[1024]{0:T(1024)}, f32[1024]{0:T(1024)S(1)}, u32[]{:S(2)}) copy-start(f32[1024]{0:T(1024)S(1)} %select_reduce_fusion.2) | copy-start | bytes 12292
  63.3 6.3 %copy-start.1 = (bf16[1,1024,4096]{2,1,0:T(8,128)(2,1)S(1)}, bf16[1,1024,4096]{2,1,0:T(8,128)(2,1)}, u32[]{:S(2)}) copy-start(bf16[1,1024,4096]{2,1,0:T(8,128)(2,1)} %param.6) | copy-start | bytes 25165828
  63.4 6.3 %copy-start.3 = (s32[1,1024]{1,0:T(1,128)S(1)}, s32[1,1024]{1,0:T(1,128)}, u32[]{:S(2)}) copy-start(s32[1,1024]{1,0:T(1,128)} %param.10) | copy-start | bytes 12292
  71.2 23.4 %copy-start.6 = (u32[256]{0:T(256)S(1)}, u32[256]{0:T(256)}, u32[]{:S(2)}) copy-start(u32[256]{0:T(256)} %constant.87) | copy-start | bytes 3076
  71.2 24.0 %copy-start.5 = (u32[256]{0:T(256)S(1)}, u32[256]{0:T(256)}, u32[]{:S(2)}) copy-start(u32[256]{0:T(256)} %constant.82) | copy-start | bytes 3076
  91.3 8.5 %all-to-all-start.1 = ((f32[8,1,8]{2,1,0:T(1,128)}), f32[8,1,8]{2,1,0:T(1,128)S(1)}, u32[]{:S(2)}, u32[]{:S(2)}) async-start(f32[8,1,8]{2,1,0:T(1,128)} %bitcast.10), calls=%async_computation.1 | async-start | bytes 8192 | tf_op jit(solution)/shard_map/all_to_all | solution.py:26
  94.5 146.0 %all-reduce.20.cloned.1.call-start = ((), (), s32[]{:S(2)}) async-start(), calls=%async_computation.3 | async-start | bytes 2105344
  173.2 1.0 copy-start.2
Sparse Core Ops, SparseCore 0:
  90.6 76.5 all-gather.16
  174.4 66.0 all-reduce.19
